TPU v7x, 32 devices: a whole 2x2x4 slice. The times are simulated.
32 devices in a mesh: pc: 8 (over z, y), pr: 4 (over x, core).
Axes of the slice: x: 2, y: 2, z: 4, core: 2. Of those that a mesh axis runs over, the one named last changes fastest.
Arguments:
- panel_in: float32 [4096, 24, 128], P('pr', 'pc')
- trail_in: float32 [4096, 1024], P('pr', 'pc')
Outputs:
- output 1: float32 [4096, 24, 128], P('pr', 'pc')
- output 2: float32 [4096, 1024], P('pr', 'pc')
All inputs are finite; a program needn't handle non-finite values.
Results may differ from a plain program's by a relative error of at most 0.001.
Values sent between devices are 32-bit elements.
A program may use at most 1 GiB of HBM per device.

v0:
```python
import jax
import jax.numpy as jnp
from jax import lax
from jax.sharding import PartitionSpec as P

PREC_HIGH = lax.Precision.HIGHEST


def solve_right(l_diag, right_side):
    return lax.linalg.triangular_solve(l_diag, right_side, left_side=False, lower=True, transpose_a=True)


def apply_update(panel_tile, trail_tile, row_panel, col_view, panel_step, row_procs, col_procs):
    local_rows, panel_dev, blk_size = panel_tile.shape
    row_start = ((panel_step + 1) // row_procs) * blk_size
    col_start = (panel_step + 1) // col_procs
    rows_part = row_panel[row_start:]
    if col_start < panel_dev:
        panel_update = jnp.einsum("rc,mbc->rmb", rows_part, col_view[col_start:panel_dev], precision=PREC_HIGH, preferred_element_type=jnp.float32)
        panel_tile = lax.dynamic_update_slice(panel_tile, panel_tile[row_start:, col_start:] - panel_update, (row_start, col_start, 0))
    trail_view = col_view[panel_dev:].reshape(trail_tile.shape[1], blk_size)
    trail_update = lax.dot_general(rows_part, trail_view, (((1,), (1,)), ((), ())), precision=PREC_HIGH, preferred_element_type=jnp.float32)
    trail_tile = lax.dynamic_update_slice(trail_tile, trail_tile[row_start:] - trail_update, (row_start, 0))
    return panel_tile, trail_tile


def solution(mesh):
    row_procs = mesh.shape["pr"]
    col_procs = mesh.shape["pc"]

    def local_part(panel_tile, trail_tile):
        local_rows, panel_dev, blk_size = panel_tile.shape
        row_blocks = local_rows // blk_size
        col_blocks = row_blocks * row_procs // col_procs
        my_row = lax.axis_index("pr")
        my_col = lax.axis_index("pc")
        block_ids = (jnp.arange(row_blocks) * row_procs + my_row)[:, None, None]
        eye_block = jnp.eye(blk_size, dtype=panel_tile.dtype)
        for panel_step in range(panel_dev * col_procs):
            owner_col = panel_step % col_procs
            local_slot = panel_step // col_procs
            owner_row = panel_step % row_procs
            diag_start = (panel_step // row_procs) * blk_size
            column = panel_tile[:, local_slot, :]
            diag_local = column[diag_start:diag_start + blk_size]
            diag_blk = lax.psum(jnp.where(my_row == owner_row, diag_local, 0.0), "pr")
            diag_blk = jnp.where(my_col == owner_col, diag_blk, eye_block)
            l_diag = jnp.linalg.cholesky(diag_blk)
            solved = solve_right(l_diag, column).reshape(row_blocks, blk_size, blk_size)
            below_diag = jnp.where(block_ids > panel_step, solved, 0.0)
            l_col = jnp.where(block_ids == panel_step, l_diag, below_diag).reshape(local_rows, blk_size)
            new_col = jnp.where(my_col == owner_col, l_col, column)
            panel_tile = lax.dynamic_update_slice(panel_tile, new_col[:, None, :], (0, local_slot, 0))
            row_panel = lax.psum(jnp.where(my_col == owner_col, below_diag.reshape(local_rows, blk_size), 0.0), "pc")
            gathered = lax.all_gather(row_panel, "pr", axis=0, tiled=False)
            by_block = gathered.reshape(row_procs, row_blocks, blk_size, blk_size).transpose(1, 0, 2, 3)
            col_view = lax.dynamic_index_in_dim(by_block.reshape(col_blocks, col_procs, blk_size, blk_size), my_col, axis=1, keepdims=False)
            panel_tile, trail_tile = apply_update(panel_tile, trail_tile, row_panel, col_view, panel_step, row_procs, col_procs)
        return panel_tile, trail_tile

    spec_panel = P("pr", "pc", None)
    spec_trail = P("pr", "pc")
    return jax.shard_map(local_part, mesh=mesh, in_specs=(spec_panel, spec_trail), out_specs=(spec_panel, spec_trail), check_vma=False)
```

profile of v0, /device:TPU:7, one launch (start us, length us, event | category | flops | bytes accessed | tf_op | source)
XLA Modules:
  0.0 3884.2 jit_solution(9392498223128843886)
XLA Ops:
  9.9 31.9 all-reduce.49.cloned.1.call-done
  66.3 71.8 %all-reduce.51.cloned.1.call-done = f32[1024,128]{0,1:T(8,128)} async-done(((f32[1024,128]{0,1:T(8,128)}), f32[1024,128]{0,1:T(8,128)}) %all-reduce.51.cloned.1.call-update) | async-done | bytes 524304 | tf_op jit(solution)/shard_map/psum | solution.py:54
  138.6 24.6 all-gather.49.cloned.1.call-done
  173.0 30.1 all-reduce.53.cloned.1.call-done
  229.4 70.1 %all-reduce.55.cloned.1.call-done = f32[1024,128]{0,1:T(8,128)} async-done(((f32[1024,128]{0,1:T(8,128)}), f32[1024,128]{0,1:T(8,128)}) %all-reduce.55.cloned.1.call-update) | async-done | bytes 524304 | tf_op jit(solution)/shard_map/psum | solution.py:54
  300.0 24.4 all-gather.51.cloned.1.call-done
  334.4 29.9 all-reduce.57.cloned.1.call-done
  388.8 71.8 %all-reduce.59.cloned.1.call-done = f32[1024,128]{0,1:T(8,128)} async-done(((f32[1024,128]{0,1:T(8,128)}), f32[1024,128]{0,1:T(8,128)}) %all-reduce.59.cloned.1.call-update) | async-done | bytes 524304 | tf_op jit(solution)/shard_map/psum | solution.py:54
  461.2 24.6 all-gather.53.cloned.1.call-done
  495.6 30.2 all-reduce.61.cloned.1.call-done
  550.3 71.8 %all-reduce.63.cloned.1.call-done = f32[1024,128]{0,1:T(8,128)} async-done(((f32[1024,128]{0,1:T(8,128)}), f32[1024,128]{0,1:T(8,128)}) %all-reduce.63.cloned.1.call-update) | async-done | bytes 524304 | tf_op jit(solution)/shard_map/psum | solution.py:54
  622.7 24.4 all-gather.55.cloned.1.call-done
  656.7 30.0 all-reduce.65.cloned.1.call-done
  711.2 71.8 %all-reduce.67.cloned.1.call-done = f32[1024,128]{0,1:T(8,128)} async-done(((f32[1024,128]{0,1:T(8,128)}), f32[1024,128]{0,1:T(8,128)}) %all-reduce.67.cloned.1.call-update) | async-done | bytes 524304 | tf_op jit(solution)/shard_map/psum | solution.py:54
  817.9 29.8 all-reduce.69.cloned.1.call-done
  872.3 72.5 %all-reduce.71.cloned.1.call-done = f32[1024,128]{0,1:T(8,128)} async-done(((f32[1024,128]{0,1:T(8,128)}), f32[1024,128]{0,1:T(8,128)}) %all-reduce.71.cloned.1.call-update) | async-done | bytes 524304 | tf_op jit(solution)/shard_map/psum | solution.py:54
  945.4 24.4 all-gather.59.cloned.1.call-done
  979.4 30.0 all-reduce.73.cloned.1.call-done
  1034.0 72.6 %all-reduce.75.cloned.1.call-done = f32[1024,128]{0,1:T(8,128)} async-done(((f32[1024,128]{0,1:T(8,128)}), f32[1024,128]{0,1:T(8,128)}) %all-reduce.75.cloned.1.call-update) | async-done | bytes 524304 | tf_op jit(solution)/shard_map/psum | solution.py:54
  1107.1 24.5 all-gather.61.cloned.1.call-done
  1141.3 30.0 all-reduce.77.cloned.1.call-done
  1195.8 73.5 %all-reduce.79.cloned.1.call-done = f32[1024,128]{0,1:T(8,128)} async-done(((f32[1024,128]{0,1:T(8,128)}), f32[1024,128]{0,1:T(8,128)}) %all-reduce.79.cloned.1.call-update) | async-done | bytes 524304 | tf_op jit(solution)/shard_map/psum | solution.py:54
  1269.9 24.4 all-gather.63.cloned.1.call-done
  1303.3 30.0 all-reduce.81.cloned.1.call-done
  1357.9 71.8 %all-reduce.83.cloned.1.call-done = f32[1024,128]{0,1:T(8,128)} async-done(((f32[1024,128]{0,1:T(8,128)}), f32[1024,128]{0,1:T(8,128)}) %all-reduce.83.cloned.1.call-update) | async-done | bytes 524304 | tf_op jit(solution)/shard_map/psum | solution.py:54
  1464.0 29.8 all-reduce.85.cloned.1.call-done
  1520.0 70.1 %all-reduce.87.cloned.1.call-done = f32[1024,128]{0,1:T(8,128)} async-done(((f32[1024,128]{0,1:T(8,128)}), f32[1024,128]{0,1:T(8,128)}) %all-reduce.87.cloned.1.call-update) | async-done | bytes 524304 | tf_op jit(solution)/shard_map/psum | solution.py:54
  1624.1 30.1 all-reduce.89.cloned.1.call-done
  1678.7 71.8 %all-reduce.91.cloned.1.call-done = f32[1024,128]{0,1:T(8,128)} async-done(((f32[1024,128]{0,1:T(8,128)}), f32[1024,128]{0,1:T(8,128)}) %all-reduce.91.cloned.1.call-update) | async-done | bytes 524304 | tf_op jit(solution)/shard_map/psum | solution.py:54
  1784.6 30.1 all-reduce.93.cloned.1.call-done
  1839.2 71.8 %all-reduce.95.cloned.1.call-done = f32[1024,128]{0,1:T(8,128)} async-done(((f32[1024,128]{0,1:T(8,128)}), f32[1024,128]{0,1:T(8,128)}) %all-reduce.95.cloned.1.call-update) | async-done | bytes 524304 | tf_op jit(solution)/shard_map/psum | solution.py:54
  1944.9 30.0 all-reduce.97.cloned.1.call-done
  1999.4 71.8 %all-reduce.99.cloned.1.call-done = f32[1024,128]{0,1:T(8,128)} async-done(((f32[1024,128]{0,1:T(8,128)}), f32[1024,128]{0,1:T(8,128)}) %all-reduce.99.cloned.1.call-update) | async-done | bytes 524304 | tf_op jit(solution)/shard_map/psum | solution.py:54
  2071.8 24.4 all-gather.73.cloned.1.call-done
  2105.4 29.8 all-reduce.101.cloned.1.call-done
  2159.8 72.6 %all-reduce.103.cloned.1.call-done = f32[1024,128]{0,1:T(8,128)} async-done(((f32[1024,128]{0,1:T(8,128)}), f32[1024,128]{0,1:T(8,128)}) %all-reduce.103.cloned.1.call-update) | async-done | bytes 524304 | tf_op jit(solution)/shard_map/psum | solution.py:54
  2232.9 24.5 all-gather.75.cloned.1.call-done
  2266.3 30.1 all-reduce.105.cloned.1.call-done
  2321.0 72.5 %all-reduce.107.cloned.1.call-done = f32[1024,128]{0,1:T(8,128)} async-done(((f32[1024,128]{0,1:T(8,128)}), f32[1024,128]{0,1:T(8,128)}) %all-reduce.107.cloned.1.call-update) | async-done | bytes 524304 | tf_op jit(solution)/shard_map/psum | solution.py:54
  2394.1 24.4 all-gather.77.cloned.1.call-done
  2427.4 30.1 all-reduce.109.cloned.1.call-done
  2482.0 73.5 %all-reduce.111.cloned.1.call-done = f32[1024,128]{0,1:T(8,128)} async-done(((f32[1024,128]{0,1:T(8,128)}), f32[1024,128]{0,1:T(8,128)}) %all-reduce.111.cloned.1.call-update) | async-done | bytes 524304 | tf_op jit(solution)/shard_map/psum | solution.py:54
  2588.9 30.1 all-reduce.113.cloned.1.call-done
  2643.8 71.8 %all-reduce.115.cloned.1.call-done = f32[1024,128]{0,1:T(8,128)} async-done(((f32[1024,128]{0,1:T(8,128)}), f32[1024,128]{0,1:T(8,128)}) %all-reduce.115.cloned.1.call-update) | async-done | bytes 524304 | tf_op jit(solution)/shard_map/psum | solution.py:54
  2715.8 24.7 all-gather.81.cloned.1.call-done
  2749.4 29.8 all-reduce.117.cloned.1.call-done
  2805.6 70.1 %all-reduce.119.cloned.1.call-done = f32[1024,128]{0,1:T(8,128)} async-done(((f32[1024,128]{0,1:T(8,128)}), f32[1024,128]{0,1:T(8,128)}) %all-reduce.119.cloned.1.call-update) | async-done | bytes 524304 | tf_op jit(solution)/shard_map/psum | solution.py:54
  2876.0 24.9 all-gather.83.cloned.1.call-done
  2909.4 30.2 all-reduce.121.cloned.1.call-done
  2964.3 71.8 %all-reduce.123.cloned.1.call-done = f32[1024,128]{0,1:T(8,128)} async-done(((f32[1024,128]{0,1:T(8,128)}), f32[1024,128]{0,1:T(8,128)}) %all-reduce.123.cloned.1.call-update) | async-done | bytes 524304 | tf_op jit(solution)/shard_map/psum | solution.py:54
  3036.3 24.9 all-gather.85.cloned.1.call-done
  3069.8 30.2 all-reduce.125.cloned.1.call-done
  3124.7 71.8 %all-reduce.127.cloned.1.call-done = f32[1024,128]{0,1:T(8,128)} async-done(((f32[1024,128]{0,1:T(8,128)}), f32[1024,128]{0,1:T(8,128)}) %all-reduce.127.cloned.1.call-update) | async-done | bytes 524304 | tf_op jit(solution)/shard_map/psum | solution.py:54
  3196.7 24.9 all-gather.87.cloned.1.call-done
  3230.1 30.1 all-reduce.129.cloned.1.call-done
  3285.0 71.8 %all-reduce.131.cloned.1.call-done = f32[1024,128]{0,1:T(8,128)} async-done(((f32[1024,128]{0,1:T(8,128)}), f32[1024,128]{0,1:T(8,128)}) %all-reduce.131.cloned.1.call-update) | async-done | bytes 524304 | tf_op jit(solution)/shard_map/psum | solution.py:54
  3357.0 24.7 all-gather.89.cloned.1.call-done
  3390.5 29.8 all-reduce.133.cloned.1.call-done
  3445.1 72.5 %all-reduce.135.cloned.1.call-done = f32[1024,128]{0,1:T(8,128)} async-done(((f32[1024,128]{0,1:T(8,128)}), f32[1024,128]{0,1:T(8,128)}) %all-reduce.135.cloned.1.call-update) | async-done | bytes 524304 | tf_op jit(solution)/shard_map/psum | solution.py:54
  3517.9 24.7 all-gather.91.cloned.1.call-done
  3551.1 30.2 all-reduce.137.cloned.1.call-done
  3606.2 72.5 %all-reduce.139.cloned.1.call-done = f32[1024,128]{0,1:T(8,128)} async-done(((f32[1024,128]{0,1:T(8,128)}), f32[1024,128]{0,1:T(8,128)}) %all-reduce.139.cloned.1.call-update) | async-done | bytes 524304 | tf_op jit(solution)/shard_map/psum | solution.py:54
  3714.3 28.3 all-reduce.141.cloned.1.call-done
  3774.8 68.1 %all-reduce.143.cloned.1.call-done = f32[1024,128]{0,1:T(8,128)} async-done(((f32[1024,128]{0,1:T(8,128)}), f32[1024,128]{0,1:T(8,128)}) %all-reduce.143.cloned.1.call-update) | async-done | bytes 524304 | tf_op jit(solution)/shard_map/psum | solution.py:54
  (742 shorter events, 1030.3 us)
Async XLA Ops:
  9.8 128.4 %all-reduce.51.cloned.1.call-start = ((), (), s32[]{:S(2)}) async-start(), calls=%async_computation.1 | async-start | bytes 1048576 | tf_op jit(solution)/shard_map/psum | solution.py:54
  66.3 96.9 %all-gather.49.cloned.1.call-start = ((), (), s32[]{:S(2)}) async-start(), calls=%async_computation.48 | async-start | bytes 2621440 | tf_op jit(solution)/shard_map/all_gather | solution.py:55
  138.1 65.0 %all-reduce.53.cloned.1.call-start = ((), (), s32[]{:S(2)}) async-start(), calls=%async_computation.2 | async-start | bytes 131072 | tf_op jit(solution)/shard_map/psum | solution.py:46
  172.7 126.8 %all-reduce.55.cloned.1.call-start = ((), (), s32[]{:S(2)}) async-start(), calls=%async_computation.3 | async-start | bytes 1048576 | tf_op jit(solution)/shard_map/psum | solution.py:54
  229.3 95.1 %all-gather.51.cloned.1.call-start = ((), (), s32[]{:S(2)}) async-start(), calls=%async_computation.49 | async-start | bytes 2621440 | tf_op jit(solution)/shard_map/all_gather | solution.py:55
  299.5 64.8 %all-reduce.57.cloned.1.call-start = ((), (), s32[]{:S(2)}) async-start(), calls=%async_computation.4 | async-start | bytes 131072 | tf_op jit(solution)/shard_map/psum | solution.py:46
  333.9 126.8 %all-reduce.59.cloned.1.call-start = ((), (), s32[]{:S(2)}) async-start(), calls=%async_computation.5 | async-start | bytes 1048576 | tf_op jit(solution)/shard_map/psum | solution.py:54
  388.8 96.9 %all-gather.53.cloned.1.call-start = ((), (), s32[]{:S(2)}) async-start(), calls=%async_computation.50 | async-start | bytes 2621440 | tf_op jit(solution)/shard_map/all_gather | solution.py:55
  460.7 65.1 %all-reduce.61.cloned.1.call-start = ((), (), s32[]{:S(2)}) async-start(), calls=%async_computation.6 | async-start | bytes 131072 | tf_op jit(solution)/shard_map/psum | solution.py:46
  495.3 126.8 %all-reduce.63.cloned.1.call-start = ((), (), s32[]{:S(2)}) async-start(), calls=%async_computation.7 | async-start | bytes 1048576 | tf_op jit(solution)/shard_map/psum | solution.py:54
  550.3 96.8 %all-gather.55.cloned.1.call-start = ((), (), s32[]{:S(2)}) async-start(), calls=%async_computation.51 | async-start | bytes 2621440 | tf_op jit(solution)/shard_map/all_gather | solution.py:55
  622.1 64.6 %all-reduce.65.cloned.1.call-start = ((), (), s32[]{:S(2)}) async-start(), calls=%async_computation.8 | async-start | bytes 131072 | tf_op jit(solution)/shard_map/psum | solution.py:46
  656.3 126.8 %all-reduce.67.cloned.1.call-start = ((), (), s32[]{:S(2)}) async-start(), calls=%async_computation.9 | async-start | bytes 1048576 | tf_op jit(solution)/shard_map/psum | solution.py:54
  711.2 96.8 %all-gather.57.cloned.1.call-start = ((), (), s32[]{:S(2)}) async-start(), calls=%async_computation.52 | async-start | bytes 2621440 | tf_op jit(solution)/shard_map/all_gather | solution.py:55
  783.1 64.7 %all-reduce.69.cloned.1.call-start = ((), (), s32[]{:S(2)}) async-start(), calls=%async_computation.10 | async-start | bytes 131072 | tf_op jit(solution)/shard_map/psum | solution.py:46
  817.3 127.5 %all-reduce.71.cloned.1.call-start = ((), (), s32[]{:S(2)}) async-start(), calls=%async_computation.11 | async-start | bytes 1048576 | tf_op jit(solution)/shard_map/psum | solution.py:54
  872.2 97.5 %all-gather.59.cloned.1.call-start = ((), (), s32[]{:S(2)}) async-start(), calls=%async_computation.53 | async-start | bytes 2621440 | tf_op jit(solution)/shard_map/all_gather | solution.py:55
  944.8 64.6 %all-reduce.73.cloned.1.call-start = ((), (), s32[]{:S(2)}) async-start(), calls=%async_computation.12 | async-start | bytes 131072 | tf_op jit(solution)/shard_map/psum | solution.py:46
  979.0 127.5 %all-reduce.75.cloned.1.call-start = ((), (), s32[]{:S(2)}) async-start(), calls=%async_computation.13 | async-start | bytes 1048576 | tf_op jit(solution)/shard_map/psum | solution.py:54
  1033.9 97.7 %all-gather.61.cloned.1.call-start = ((), (), s32[]{:S(2)}) async-start(), calls=%async_computation.54 | async-start | bytes 2621440 | tf_op jit(solution)/shard_map/all_gather | solution.py:55
  1106.6 64.7 %all-reduce.77.cloned.1.call-start = ((), (), s32[]{:S(2)}) async-start(), calls=%async_computation.14 | async-start | bytes 131072 | tf_op jit(solution)/shard_map/psum | solution.py:46
  1140.8 128.5 %all-reduce.79.cloned.1.call-start = ((), (), s32[]{:S(2)}) async-start(), calls=%async_computation.15 | async-start | bytes 1048576 | tf_op jit(solution)/shard_map/psum | solution.py:54
  1195.7 98.5 %all-gather.63.cloned.1.call-start = ((), (), s32[]{:S(2)}) async-start(), calls=%async_computation.55 | async-start | bytes 2621440 | tf_op jit(solution)/shard_map/all_gather | solution.py:55
  1269.3 64.1 %all-reduce.81.cloned.1.call-start = ((), (), s32[]{:S(2)}) async-start(), calls=%async_computation.16 | async-start | bytes 131072 | tf_op jit(solution)/shard_map/psum | solution.py:46
  1302.9 126.8 %all-reduce.83.cloned.1.call-start = ((), (), s32[]{:S(2)}) async-start(), calls=%async_computation.17 | async-start | bytes 1048576 | tf_op jit(solution)/shard_map/psum | solution.py:54
  1357.8 96.8 %all-gather.65.cloned.1.call-start = ((), (), s32[]{:S(2)}) async-start(), calls=%async_computation.56 | async-start | bytes 2621440 | tf_op jit(solution)/shard_map/all_gather | solution.py:55
  1429.7 64.1 %all-reduce.85.cloned.1.call-start = ((), (), s32[]{:S(2)}) async-start(), calls=%async_computation.18 | async-start | bytes 131072 | tf_op jit(solution)/shard_map/psum | solution.py:46
  1463.3 126.8 %all-reduce.87.cloned.1.call-start = ((), (), s32[]{:S(2)}) async-start(), calls=%async_computation.19 | async-start | bytes 1048576 | tf_op jit(solution)/shard_map/psum | solution.py:54
  1519.9 95.1 %all-gather.67.cloned.1.call-start = ((), (), s32[]{:S(2)}) async-start(), calls=%async_computation.57 | async-start | bytes 2621440 | tf_op jit(solution)/shard_map/all_gather | solution.py:55
  1590.1 64.1 %all-reduce.89.cloned.1.call-start = ((), (), s32[]{:S(2)}) async-start(), calls=%async_computation.20 | async-start | bytes 131072 | tf_op jit(solution)/shard_map/psum | solution.py:46
  1623.8 126.8 %all-reduce.91.cloned.1.call-start = ((), (), s32[]{:S(2)}) async-start(), calls=%async_computation.21 | async-start | bytes 1048576 | tf_op jit(solution)/shard_map/psum | solution.py:54
  1678.7 96.8 %all-gather.69.cloned.1.call-start = ((), (), s32[]{:S(2)}) async-start(), calls=%async_computation.58 | async-start | bytes 2621440 | tf_op jit(solution)/shard_map/all_gather | solution.py:55
  1750.5 64.1 %all-reduce.93.cloned.1.call-start = ((), (), s32[]{:S(2)}) async-start(), calls=%async_computation.22 | async-start | bytes 131072 | tf_op jit(solution)/shard_map/psum | solution.py:46
  1784.2 126.8 %all-reduce.95.cloned.1.call-start = ((), (), s32[]{:S(2)}) async-start(), calls=%async_computation.23 | async-start | bytes 1048576 | tf_op jit(solution)/shard_map/psum | solution.py:54
  1839.1 96.8 %all-gather.71.cloned.1.call-start = ((), (), s32[]{:S(2)}) async-start(), calls=%async_computation.59 | async-start | bytes 2621440 | tf_op jit(solution)/shard_map/all_gather | solution.py:55
  1911.0 63.9 %all-reduce.97.cloned.1.call-start = ((), (), s32[]{:S(2)}) async-start(), calls=%async_computation.24 | async-start | bytes 131072 | tf_op jit(solution)/shard_map/psum | solution.py:46
  1944.5 126.7 %all-reduce.99.cloned.1.call-start = ((), (), s32[]{:S(2)}) async-start(), calls=%async_computation.25 | async-start | bytes 1048576 | tf_op jit(solution)/shard_map/psum | solution.py:54
  1999.4 96.8 %all-gather.73.cloned.1.call-start = ((), (), s32[]{:S(2)}) async-start(), calls=%async_computation.60 | async-start | bytes 2621440 | tf_op jit(solution)/shard_map/all_gather | solution.py:55
  2071.3 64.0 %all-reduce.101.cloned.1.call-start = ((), (), s32[]{:S(2)}) async-start(), calls=%async_computation.26 | async-start | bytes 131072 | tf_op jit(solution)/shard_map/psum | solution.py:46
  2104.9 127.5 %all-reduce.103.cloned.1.call-start = ((), (), s32[]{:S(2)}) async-start(), calls=%async_computation.27 | async-start | bytes 1048576 | tf_op jit(solution)/shard_map/psum | solution.py:54
  2159.7 97.7 %all-gather.75.cloned.1.call-start = ((), (), s32[]{:S(2)}) async-start(), calls=%async_computation.61 | async-start | bytes 2621440 | tf_op jit(solution)/shard_map/all_gather | solution.py:55
  2232.4 64.1 %all-reduce.105.cloned.1.call-start = ((), (), s32[]{:S(2)}) async-start(), calls=%async_computation.28 | async-start | bytes 131072 | tf_op jit(solution)/shard_map/psum | solution.py:46
  2266.0 127.5 %all-reduce.107.cloned.1.call-start = ((), (), s32[]{:S(2)}) async-start(), calls=%async_computation.29 | async-start | bytes 1048576 | tf_op jit(solution)/shard_map/psum | solution.py:54
  2321.0 97.5 %all-gather.77.cloned.1.call-start = ((), (), s32[]{:S(2)}) async-start(), calls=%async_computation.62 | async-start | bytes 2621440 | tf_op jit(solution)/shard_map/all_gather | solution.py:55
  2393.6 63.9 %all-reduce.109.cloned.1.call-start = ((), (), s32[]{:S(2)}) async-start(), calls=%async_computation.30 | async-start | bytes 131072 | tf_op jit(solution)/shard_map/psum | solution.py:46
  2427.0 128.4 %all-reduce.111.cloned.1.call-start = ((), (), s32[]{:S(2)}) async-start(), calls=%async_computation.31 | async-start | bytes 1048576 | tf_op jit(solution)/shard_map/psum | solution.py:54
  2481.9 98.5 %all-gather.79.cloned.1.call-start = ((), (), s32[]{:S(2)}) async-start(), calls=%async_computation.63 | async-start | bytes 2621440 | tf_op jit(solution)/shard_map/all_gather | solution.py:55
  2588.6 127.0 %all-reduce.115.cloned.1.call-start = ((), (), s32[]{:S(2)}) async-start(), calls=%async_computation.33 | async-start | bytes 1048576 | tf_op jit(solution)/shard_map/psum | solution.py:54
  2643.7 96.8 %all-gather.81.cloned.1.call-start = ((), (), s32[]{:S(2)}) async-start(), calls=%async_computation.64 | async-start | bytes 2621440 | tf_op jit(solution)/shard_map/all_gather | solution.py:55
  2748.8 127.0 %all-reduce.119.cloned.1.call-start = ((), (), s32[]{:S(2)}) async-start(), calls=%async_computation.35 | async-start | bytes 1048576 | tf_op jit(solution)/shard_map/psum | solution.py:54
  2805.6 95.3 %all-gather.83.cloned.1.call-start = ((), (), s32[]{:S(2)}) async-start(), calls=%async_computation.65 | async-start | bytes 2621440 | tf_op jit(solution)/shard_map/all_gather | solution.py:55
  2909.1 127.0 %all-reduce.123.cloned.1.call-start = ((), (), s32[]{:S(2)}) async-start(), calls=%async_computation.37 | async-start | bytes 1048576 | tf_op jit(solution)/shard_map/psum | solution.py:54
  2964.2 96.9 %all-gather.85.cloned.1.call-start = ((), (), s32[]{:S(2)}) async-start(), calls=%async_computation.66 | async-start | bytes 2621440 | tf_op jit(solution)/shard_map/all_gather | solution.py:55
  3069.4 127.1 %all-reduce.127.cloned.1.call-start = ((), (), s32[]{:S(2)}) async-start(), calls=%async_computation.39 | async-start | bytes 1048576 | tf_op jit(solution)/shard_map/psum | solution.py:54
  3124.6 96.9 %all-gather.87.cloned.1.call-start = ((), (), s32[]{:S(2)}) async-start(), calls=%async_computation.67 | async-start | bytes 2621440 | tf_op jit(solution)/shard_map/all_gather | solution.py:55
  3229.8 127.0 %all-reduce.131.cloned.1.call-start = ((), (), s32[]{:S(2)}) async-start(), calls=%async_computation.41 | async-start | bytes 1048576 | tf_op jit(solution)/shard_map/psum | solution.py:54
  3284.9 96.8 %all-gather.89.cloned.1.call-start = ((), (), s32[]{:S(2)}) async-start(), calls=%async_computation.68 | async-start | bytes 2621440 | tf_op jit(solution)/shard_map/all_gather | solution.py:55
  3389.9 127.8 %all-reduce.135.cloned.1.call-start = ((), (), s32[]{:S(2)}) async-start(), calls=%async_computation.43 | async-start | bytes 1048576 | tf_op jit(solution)/shard_map/psum | solution.py:54
  3445.1 97.5 %all-gather.91.cloned.1.call-start = ((), (), s32[]{:S(2)}) async-start(), calls=%async_computation.69 | async-start | bytes 2621440 | tf_op jit(solution)/shard_map/all_gather | solution.py:55
  3550.8 128.0 %all-reduce.139.cloned.1.call-start = ((), (), s32[]{:S(2)}) async-start(), calls=%async_computation.45 | async-start | bytes 1048576 | tf_op jit(solution)/shard_map/psum | solution.py:54
  3606.1 97.7 %all-gather.93.cloned.1.call-start = ((), (), s32[]{:S(2)}) async-start(), calls=%async_computation.70 | async-start | bytes 2621440 | tf_op jit(solution)/shard_map/all_gather | solution.py:55
  3678.8 63.8 %all-reduce.141.cloned.1.call-start = ((), (), s32[]{:S(2)}) async-start(), calls=%async_computation.46 | async-start | bytes 131072 | tf_op jit(solution)/shard_map/psum | solution.py:46
  3712.2 130.7 %all-reduce.143.cloned.1.call-start = ((), (), s32[]{:S(2)}) async-start(), calls=%async_computation.47 | async-start | bytes 1048576 | tf_op jit(solution)/shard_map/psum | solution.py:54
  3769.4 99.6 %all-gather.95.cloned.1.call-start = ((), (), s32[]{:S(2)}) async-start(), calls=%async_computation.71 | async-start | bytes 2621440 | tf_op jit(solution)/shard_map/all_gather | solution.py:55
  (47 other events, 1043.0 us)
Sparse Core Ops, SparseCore 0:
  10.9 30.8 all-reduce.48
  66.4 71.6 all-reduce.50
  139.7 23.4 all-gather.48
  172.8 30.3 all-reduce.52
  229.4 70.0 all-reduce.54
  300.9 23.4 all-gather.50
  334.0 30.2 all-reduce.56
  388.9 71.6 all-reduce.58
  462.2 23.4 all-gather.52
  495.5 30.2 all-reduce.60
  550.4 71.6 all-reduce.62
  623.5 23.4 all-gather.54
  656.4 30.2 all-reduce.64
  711.3 71.6 all-reduce.66
  784.5 23.4 all-gather.56
  817.4 30.2 all-reduce.68
  872.3 72.4 all-reduce.70
  946.2 23.4 all-gather.58
  979.2 30.2 all-reduce.72
  1034.1 72.4 all-reduce.74
  1108.1 23.4 all-gather.60
  1140.9 30.2 all-reduce.76
  1195.9 73.3 all-reduce.78
  1270.7 23.4 all-gather.62
  1303.1 30.2 all-reduce.80
  1358.0 71.6 all-reduce.82
  1431.1 23.4 all-gather.64
  1463.5 30.2 all-reduce.84
  1520.0 70.0 all-reduce.86
  1591.5 23.4 all-gather.66
  1623.9 30.2 all-reduce.88
  1678.8 71.6 all-reduce.90
  1751.9 23.4 all-gather.68
  1784.3 30.2 all-reduce.92
  1839.2 71.6 all-reduce.94
  1912.4 23.4 all-gather.70
  1944.6 30.2 all-reduce.96
  1999.5 71.6 all-reduce.98
  2072.7 23.4 all-gather.72
  2105.0 30.2 all-reduce.100
  2159.9 72.4 all-reduce.102
  2233.9 23.4 all-gather.74
  2266.2 30.2 all-reduce.104
  2321.1 72.4 all-reduce.106
  2395.0 23.4 all-gather.76
  2427.1 30.2 all-reduce.108
  2482.1 73.3 all-reduce.110
  2588.7 30.2 all-reduce.112
  2643.9 71.6 all-reduce.114
  2748.9 30.2 all-reduce.116
  2805.7 70.0 all-reduce.118
  2909.2 30.2 all-reduce.120
  2964.4 71.6 all-reduce.122
  3069.5 30.3 all-reduce.124
  3124.8 71.6 all-reduce.126
  3229.9 30.2 all-reduce.128
  3285.1 71.6 all-reduce.130
  3390.0 30.2 all-reduce.132
  3445.2 72.4 all-reduce.134
  3550.9 30.2 all-reduce.136
  3606.3 72.4 all-reduce.138
  3680.3 23.4 all-gather.92
  3712.3 30.2 all-reduce.140
  3769.5 73.3 all-reduce.142
  (8 shorter events, 187.5 us)
where the time goes:
time: 3900 us; the launch traced here: 3880 us
  waiting for transfers between devices  2990 us (77%)
  other arithmetic  574 us (15%)
  local copies, waits for them, and re-layouts  167 us (4%)
  matrix products  124 us (3%)
    psum x24, waiting for transfers between devices, local_part(): lax.psum(jnp.where(my_col == owner_col, below_diag.reshape(local_rows, bl...  1720 us
    psum x24, waiting for transfers between devices, local_part(): diag_blk = lax.psum(jnp.where(my_row == owner_row, diag_local, 0.0), 'pr')  721 us
    all_gather x24, waiting for transfers between devices, local_part(): gathered = lax.all_gather(row_panel, 'pr', axis=0, tiled=False)  548 us
    another operation x72, other arithmetic, local_part(): l_diag = jnp.linalg.cholesky(diag_blk)  297 us
    another operation x48, other arithmetic, solve_right(): lax.linalg.triangular_solve(l_diag, right_side, left_side=False, lower=Tr...  252 us
    unnamed x104, local copies, waits for them, and re-layouts  83.6 us
  transfers between devices with their start and end apart: 72, of which 71 were waited for; matrix products, arithmetic and copies ran while one was open for 2% of the time, Pallas kernels for 0%

commit v1 on v0

v1 whole, which is shorter than its diff:
```python
import jax
import jax.numpy as jnp
from jax import lax
from jax.experimental import pallas as pl
from jax.experimental.pallas import tpu as pltpu
from jax.sharding import PartitionSpec as P

MESH = pl.DeviceIdType.MESH
PREC_HIGH = lax.Precision.HIGHEST
NB = 128
LAG = 3
CHAIN_COL = 2
CHAIN_ROW = 1
RING = 8


def _sub_bcast(v, s):
    return jnp.broadcast_to(v[s:s + 1, :], (8, NB))


def _lane_bcast(v, c):
    return jnp.broadcast_to(v[:, c:c + 1], (8, NB))


def chol_inv(load, store_l, store_inv, q=2):
    ng = NB // 8
    step = 8 * q
    x = [load(g) for g in range(ng)]
    row_id = lax.broadcasted_iota(jnp.int32, (8, NB), 0)
    col_id = lax.broadcasted_iota(jnp.int32, (8, NB), 1)
    y = [jnp.where(col_id == row_id + 8 * g, 1.0, 0.0) for g in range(ng)]
    for b in range(NB // step):
        g0 = b * q
        c0 = b * step
        last = b == NB // step - 1
        e = [[_lane_bcast(x[g0 + s], c0 + t) if 8 * (s + 1) > t else None for s in range(q)] for t in range(step)]
        p = None
        if not last:
            p = [[_lane_bcast(x[g0 + q + s], c0 + t) for s in range(q)] for t in range(step)]
        rr = [None] * q
        ss = [None] * q
        rows = []
        for t in range(step):
            gt, st = t // 8, t % 8
            d = _sub_bcast(e[t][gt], st)
            r = lax.rsqrt(d)
            col = [e[t][s] * r if s >= gt else None for s in range(q)]
            rt = _sub_bcast(x[g0 + gt], st) * r
            sr = _sub_bcast(y[g0 + gt], st) * r
            rows.append((rt, sr))
            if st == 0:
                rr[gt], ss[gt] = rt, sr
            else:
                rr[gt] = jnp.where(row_id == st, rt, rr[gt])
                ss[gt] = jnp.where(row_id == st, sr, ss[gt])
            for s in range(gt, q):
                x[g0 + s] = x[g0 + s] - col[s] * rt
                y[g0 + s] = y[g0 + s] - col[s] * sr
            pc = None
            if not last:
                pc = [p[t][s] * r for s in range(q)]
                for s in range(q):
                    x[g0 + q + s] = x[g0 + q + s] - pc[s] * rt
                    y[g0 + q + s] = y[g0 + q + s] - pc[s] * sr
            for u in range(t + 1, step):
                w = _sub_bcast(col[u // 8], u % 8)
                for s in range(u // 8, q):
                    e[u][s] = e[u][s] - col[s] * w
                if not last:
                    for s in range(q):
                        p[u][s] = p[u][s] - pc[s] * w
        for s in range(q):
            store_l(g0 + s, jnp.where(col_id >= row_id + 8 * (g0 + s), rr[s], 0.0))
            store_inv(g0 + s, jnp.where(col_id <= row_id + 8 * (g0 + s), ss[s], 0.0))
        if b < NB // step - 2:
            for s in range(q):
                rt_t = jnp.transpose(rr[s])
                for g in range(g0 + 2 * q, ng):
                    blk = rt_t[8 * g:8 * g + 8, :]
                    for st in range(8):
                        m = jnp.broadcast_to(blk[:, st:st + 1], (8, NB))
                        rt, sr = rows[8 * s + st]
                        x[g] = x[g] - m * rt
                        y[g] = y[g] - m * sr


def dot_nt(a, b):
    return lax.dot_general(a, b, (((1,), (1,)), ((), ())), precision=PREC_HIGH, preferred_element_type=jnp.float32)


def make_kernel(row_procs, col_procs, local_rows, panel_dev):
    steps = panel_dev * col_procs
    row_blocks = local_rows // NB
    slots = panel_dev + 1
    half = row_blocks // 2
    sib_row = CHAIN_ROW ^ 1

    def kernel(pan_in, trl_in, pan_out, trl_out, tile, rowp, colp, linv_in, ldiag_in, stage, win, lwin, linv_c, lt_c, diag,
               in_sem, row_sem, col_sem, linv_sem, ldiag_sem, win_sem, outc_sem, out_sem,
               row_snd, col_snd, stage_snd, init_snd, linv_snd, ldiag_snd, give_snd, give_sem):
        pc = lax.axis_index("pc")
        pr = lax.axis_index("pr")
        at_chain_col = pc == CHAIN_COL
        is_chain = jnp.logical_and(at_chain_col, pr == CHAIN_ROW)
        is_sib = jnp.logical_and(at_chain_col, pr == sib_row)
        chain_id = (CHAIN_COL, CHAIN_ROW)
        sib_id = (CHAIN_COL, sib_row)
        some_other = (pc, pr ^ 1)

        def rows(l):
            return pl.ds(pl.multiple_of(l * NB, NB), NB)

        def remote(src, dst, snd, rcv, dev):
            return pltpu.make_async_remote_copy(src_ref=src, dst_ref=dst, send_sem=snd, recv_sem=rcv, device_id=dev, device_id_type=MESH)

        def wait_recv(ref, rcv):
            remote(ref, ref, give_snd.at[0], rcv, some_other).wait_recv()

        barrier = pltpu.get_barrier_semaphore()
        total = row_procs * col_procs
        me = pc * row_procs + pr

        def greet(d, _):
            other = lax.rem(me + d, total)
            pl.semaphore_signal(barrier, inc=1, device_id=(other // row_procs, lax.rem(other, row_procs)), device_id_type=MESH)
            return 0

        def load(m):
            src = pan_in.at[m] if m < panel_dev else trl_in
            return pltpu.make_async_copy(src, tile.at[0, m], in_sem.at[m])

        @pl.when(jnp.logical_not(is_chain))
        def _():
            for m in range(slots):
                load(m).start()

        lax.fori_loop(1, total, greet, 0)
        pl.semaphore_wait(barrier, total - 1)

        def give(m):
            src = pan_in.at[m] if m < panel_dev else trl_in
            return remote(src, tile.at[1, m], give_snd.at[m], give_sem.at[m], sib_id)

        def linv_copy(i, r):
            return remote(linv_c.at[lax.rem(i, RING)], linv_in.at[i // col_procs], linv_snd.at[lax.rem(i, 2), r], linv_sem.at[i // col_procs],
                          (lax.rem(i, col_procs), r))

        def linv_goes(i, r):
            return jnp.logical_or(lax.rem(i, col_procs) != CHAIN_COL, r != CHAIN_ROW)

        def ldiag_copy(i):
            return remote(lt_c.at[i], ldiag_in.at[i // col_procs], ldiag_snd.at[lax.rem(i, 2)], ldiag_sem.at[i // col_procs],
                          (lax.rem(i, col_procs), lax.rem(i, row_procs)))

        def drain_chain(i):
            for r in range(row_procs):
                @pl.when(linv_goes(i, r))
                def _():
                    linv_copy(i, r).wait_send()
            ldiag_copy(i).wait_send()

        def chain_step(i, _):
            for s in range(LAG + 1):
                @pl.when(i - LAG + s >= 0)
                def _():
                    wait_recv(win.at[i, s], win_sem.at[i, s])
            at = lax.rem(i, RING)
            old = [lax.rem(i + RING - LAG + s, RING) for s in range(LAG)]
            for s in range(LAG):
                acc = win[i, s]
                for q in range(s):
                    acc = acc - dot_nt(lwin[at, q], lwin[old[s], LAG - s + q])
                lwin[at, s] = dot_nt(acc, linv_c[old[s]])
            new_diag = win[i, LAG]
            for s in range(LAG):
                new_diag = new_diag - dot_nt(lwin[at, s], lwin[at, s])
            diag[...] = new_diag

            def put_l(g, v):
                lt_c[i, 8 * g:8 * g + 8, :] = v

            def put_inv(g, v):
                linv_c[at, 8 * g:8 * g + 8, :] = v

            chol_inv(lambda g: diag[8 * g:8 * g + 8, :], put_l, put_inv)

            @pl.when(i >= 2)
            def _():
                drain_chain(i - 2)

            for r in range(row_procs):
                @pl.when(linv_goes(i, r))
                def _():
                    linv_copy(i, r).start()
            ldiag_copy(i).start()
            return 0

        @pl.when(is_chain)
        def _():
            for m in range(slots):
                give(m).start()
            for i in range(RING):
                linv_c[i] = jnp.zeros((NB, NB), jnp.float32)
                for s in range(LAG):
                    lwin[i, s] = jnp.zeros((NB, NB), jnp.float32)
            for i in range(LAG):
                for s in range(LAG - i):
                    win[i, s] = jnp.zeros((NB, NB), jnp.float32)
            lax.fori_loop(0, steps, chain_step, 0)
            drain_chain(steps - 2)
            drain_chain(steps - 1)
            for m in range(slots):
                give(m).wait_send()
            for m in range(slots):
                dst = pan_out.at[m] if m < panel_dev else trl_out
                wait_recv(dst, outc_sem.at[m])

        num_virtual = jnp.where(is_sib, 2, 1)
        col_half = pc // row_procs
        z_me, y_me = pc // 2, lax.rem(pc, 2)
        is_col_src = pr == lax.rem(pc, row_procs)

        def row_of(v):
            return jnp.where(v == 0, pr, CHAIN_ROW)

        def first_block(k, r):
            return (k - r + row_procs) // row_procs

        def row_children(k):
            owner = lax.rem(k, col_procs)
            z_own, y_own = owner // 2, lax.rem(owner, 2)
            to_y = pc == owner
            to_up = jnp.logical_and(z_me >= z_own, z_me < col_procs // 2 - 1)
            to_down = jnp.logical_and(z_me <= z_own, z_me > 0)
            return ((to_y, z_me * 2 + 1 - y_me), (to_up, pc + 2), (to_down, pc - 2))

        def row_copy(k, v, l, c, peer):
            r = row_of(v)
            moved = jnp.logical_and(peer == CHAIN_COL, r == CHAIN_ROW)
            v_dst = jnp.where(moved, 1, 0)
            r_dst = jnp.where(moved, sib_row, r)
            return remote(rowp.at[v, k, rows(l)], rowp.at[v_dst, k, rows(l)], row_snd.at[lax.rem(k, 2), v, l, c],
                          row_sem.at[v_dst, k, l], (peer, r_dst))

        def col_copy(k, v, l, m, d):
            return remote(rowp.at[v, k, rows(l)], colp.at[k, rows(m)], col_snd.at[lax.rem(k, 2), m, d - 1],
                          col_sem.at[k, m], (pc, lax.rem(pr + d, row_procs)))

        def col_goes(d):
            return jnp.logical_not(jnp.logical_and(at_chain_col, lax.rem(pr + d, row_procs) == CHAIN_ROW))

        def is_col_block(v, l):
            return jnp.logical_and(row_of(v) == lax.rem(pc, row_procs), lax.rem(l, 2) == col_half)

        def each_block(k, act):
            def virtual(v, _):
                def block(l, _):
                    act(v, l)
                    return 0
                return lax.fori_loop(first_block(k, row_of(v)), row_blocks, block, 0)
            lax.fori_loop(0, num_virtual, virtual, 0)

        def each_send(k, v, l, act):
            for c, (goes, peer) in enumerate(row_children(k)):
                @pl.when(goes)
                def _():
                    act(row_copy(k, v, l, c, peer))

            @pl.when(is_col_block(v, l))
            def _():
                for d in range(1, row_procs):
                    @pl.when(col_goes(d))
                    def _():
                        act(col_copy(k, v, l, l // 2, d))

        def drain_sends(k):
            each_block(k, lambda v, l: each_send(k, v, l, lambda c: c.wait_send()))

        def stage_copy(v, i, s):
            return remote(stage.at[v, i // row_procs], win.at[i, s], stage_snd.at[v, i // row_procs], win_sem.at[i, s], chain_id)

        def entering(k, v):
            i = k + LAG + 1
            s = lax.rem(pc - (k + 1) + 4 * col_procs, col_procs)
            here = jnp.logical_and(jnp.logical_and(i < steps, s <= LAG), row_of(v) == lax.rem(i, row_procs))
            return here, i, s, (k + 1 + s) // col_procs

        def init_copy(i):
            return remote(pan_in.at[0, pl.ds((i // row_procs) * NB, NB)], win.at[i, jnp.clip(pc - i + LAG, 0, LAG)], init_snd.at[i],
                          win_sem.at[i, jnp.clip(pc - i + LAG, 0, LAG)], chain_id)

        def init_goes(i):
            return jnp.logical_and(pr == i % row_procs, pc <= i)

        def out_local(m):
            dst = pan_out.at[m] if m < panel_dev else trl_out
            return pltpu.make_async_copy(tile.at[0, m], dst, out_sem.at[m])

        def out_remote(m):
            dst = pan_out.at[m] if m < panel_dev else trl_out
            return remote(tile.at[1, m], dst, out_sem.at[slots + m], outc_sem.at[m], chain_id)

        def start_out(m):
            out_local(m).start()

            @pl.when(is_sib)
            def _():
                out_remote(m).start()

        def owner_step(k, _):
            own = pc == lax.rem(k, col_procs)
            m_own = k // col_procs

            @pl.when(k >= 2)
            def _():
                drain_sends(k - 2)

            @pl.when(own)
            def _():
                wait_recv(linv_in.at[m_own], linv_sem.at[m_own])

            def panel(v, l):
                @pl.when(own)
                def _():
                    x = dot_nt(tile[v, m_own, rows(l), :], linv_in[m_own])
                    rowp[v, k, rows(l), :] = x
                    tile[v, m_own, rows(l), :] = x

                @pl.when(jnp.logical_not(own))
                def _():
                    wait_recv(rowp.at[v, k, rows(l)], row_sem.at[v, k, l])

                each_send(k, v, l, lambda c: c.start())

                @pl.when(is_col_block(v, l))
                def _():
                    colp[k, rows(l // 2), :] = rowp[v, k, rows(l), :]

            each_block(k, panel)

            has_src = jnp.logical_or(is_col_src, jnp.logical_and(is_sib, CHAIN_ROW == lax.rem(pc, row_procs)))
            for m in range(slots):
                @pl.when(jnp.logical_and(jnp.logical_not(has_src), pc + m * col_procs > k))
                def _():
                    wait_recv(colp.at[k, m * NB:(m + 1) * NB], col_sem.at[k, m])

            def enter(v, _):
                here, i, s, m = entering(k, v)

                @pl.when(here)
                def _():
                    l = i // row_procs
                    new = tile[v, m, rows(l), :] - dot_nt(rowp[v, k, rows(l), :], colp[k, rows(m), :])
                    tile[v, m, rows(l), :] = new
                    stage[v, l] = new
                    stage_copy(v, i, s).start()
                return 0

            lax.fori_loop(0, num_virtual, enter, 0)

            def update(v, _):
                r = row_of(v)
                here, i, s, m_in = entering(k, v)
                l_in = jnp.where(here, i // row_procs, -1)
                first = first_block(k, r)
                for m in range(slots):
                    col_block = pc + m * col_procs
                    low = first
                    if m < panel_dev:
                        low = jnp.maximum(first, (col_block - r + row_procs - 1) // row_procs)
                    for h in range(2):
                        @pl.when(jnp.logical_and(col_block > k, low < (h + 1) * half))
                        def _():
                            part = pl.ds(h * half * NB, half * NB)
                            upd = dot_nt(rowp[v, k, part, :], colp[k, m * NB:(m + 1) * NB, :])
                            for b in range(half):
                                l = h * half + b
                                take = jnp.logical_and(l >= low, jnp.logical_or(m_in != m, l_in != l))
                                blk = slice(l * NB, (l + 1) * NB)
                                tile[v, m, blk, :] = tile[v, m, blk, :] - jnp.where(take, upd[b * NB:(b + 1) * NB], 0.0)
                return 0

            lax.fori_loop(0, num_virtual, update, 0)

            @pl.when(own)
            def _():
                def finish(v, _):
                    r = row_of(v)

                    @pl.when(r == lax.rem(k, row_procs))
                    def _():
                        wait_recv(ldiag_in.at[m_own], ldiag_sem.at[m_own])
                        tile[v, m_own, rows(k // row_procs), :] = jnp.transpose(ldiag_in[m_own])

                    def clear(l, _):
                        tile[v, m_own, rows(l), :] = jnp.zeros((NB, NB), jnp.float32)
                        return 0

                    lax.fori_loop(0, (k - r + row_procs - 1) // row_procs, clear, 0)
                    return 0

                lax.fori_loop(0, num_virtual, finish, 0)
                for m in range(panel_dev):
                    @pl.when(m_own == m)
                    def _():
                        start_out(m)
            return 0

        @pl.when(jnp.logical_not(is_chain))
        def _():
            for i in range(LAG + 1):
                @pl.when(init_goes(i))
                def _():
                    init_copy(i).start()
            for m in range(slots):
                load(m).wait()

            @pl.when(is_sib)
            def _():
                for m in range(slots):
                    wait_recv(tile.at[1, m], give_sem.at[m])

            lax.fori_loop(0, steps, owner_step, 0)
            start_out(panel_dev)
            drain_sends(steps - 2)
            drain_sends(steps - 1)
            for i in range(LAG + 1):
                @pl.when(init_goes(i))
                def _():
                    init_copy(i).wait_send()

            def drain_stage(k, _):
                def virtual(v, _):
                    here, i, s, m = entering(k, v)

                    @pl.when(here)
                    def _():
                        stage_copy(v, i, s).wait_send()
                    return 0
                return lax.fori_loop(0, num_virtual, virtual, 0)

            lax.fori_loop(0, steps, drain_stage, 0)
            for m in range(slots):
                out_local(m).wait()

                @pl.when(is_sib)
                def _():
                    out_remote(m).wait_send()

    return kernel


def solution(mesh):
    row_procs = mesh.shape["pr"]
    col_procs = mesh.shape["pc"]

    def local_part(panel_tile, trail_tile):
        local_rows, panel_dev, _ = panel_tile.shape
        steps = panel_dev * col_procs
        row_blocks = local_rows // NB
        slots = panel_dev + 1
        f32 = jnp.float32
        dma = pltpu.SemaphoreType.DMA
        scratch = [
            pltpu.VMEM((2, slots, local_rows, NB), f32),
            pltpu.VMEM((2, steps, local_rows, NB), f32),
            pltpu.VMEM((steps, slots * NB, NB), f32),
            pltpu.VMEM((panel_dev, NB, NB), f32),
            pltpu.VMEM((panel_dev, NB, NB), f32),
            pltpu.VMEM((2, steps // row_procs, NB, NB), f32),
            pltpu.VMEM((steps, LAG + 1, NB, NB), f32),
            pltpu.VMEM((RING, LAG, NB, NB), f32),
            pltpu.VMEM((RING, NB, NB), f32),
            pltpu.VMEM((steps, NB, NB), f32),
            pltpu.VMEM((NB, NB), f32),
            dma((slots,)),
            dma((2, steps, row_blocks)),
            dma((steps, slots)),
            dma((panel_dev,)),
            dma((panel_dev,)),
            dma((steps, LAG + 1)),
            dma((slots,)),
            dma((2 * slots,)),
            dma((2, 2, row_blocks, 3)),
            dma((2, slots, row_procs - 1)),
            dma((2, steps // row_procs)),
            dma((LAG + 1,)),
            dma((2, row_procs)),
            dma((2,)),
            dma((slots,)),
            dma((slots,)),
        ]
        hbm = pl.BlockSpec(memory_space=pl.ANY)
        by_slot = jnp.transpose(panel_tile, (1, 0, 2))
        panel_new, trail_new = pl.pallas_call(
            make_kernel(row_procs, col_procs, local_rows, panel_dev),
            out_shape=[jax.ShapeDtypeStruct(by_slot.shape, f32), jax.ShapeDtypeStruct(trail_tile.shape, f32)],
            in_specs=[hbm, hbm],
            out_specs=[hbm, hbm],
            scratch_shapes=scratch,
            compiler_params=pltpu.CompilerParams(collective_id=0, has_side_effects=True, vmem_limit_bytes=67043328),
        )(by_slot, trail_tile)
        return jnp.transpose(panel_new, (1, 0, 2)), trail_new

    spec_panel = P("pr", "pc", None)
    spec_trail = P("pr", "pc")
    return jax.shard_map(local_part, mesh=mesh, in_specs=(spec_panel, spec_trail), out_specs=(spec_panel, spec_trail), check_vma=False)
```

time: 3900 us -> 398 us (0.10)
  waiting for transfers between devices: 2990 us -> 0 us
  other arithmetic: 574 us -> 0 us
  Pallas kernels: 0 us -> 388 us
  local copies, waits for them, and re-layouts: 167 us -> 3.51 us
  matrix products: 124 us -> 0 us
    psum x48 -> x0, waiting for transfers between devices: 2440 us -> none  [the longest x24 1720 us: local_part(): lax.psum(jnp.where(my_col == owner_col, below_diag.reshape(local_rows, bl...]
    another operation x120 -> x0, other arithmetic: 550 us -> none  [the longest x72 297 us: local_part(): l_diag = jnp.linalg.cholesky(diag_blk)]
    all_gather x24 -> x0, waiting for transfers between devices: 548 us -> none  [local_part(): gathered = lax.all_gather(row_panel, 'pr', axis=0, tiled=False)]
    pallas_call x0 -> x1, Pallas kernels: none -> 388 us  [local_part(): pl.pallas_call(make_kernel(row_procs, col_procs, local_rows, panel_dev),...]
    dot_general x47 -> x0, matrix products: 87.9 us -> none  [the longest x24 48.2 us: apply_update(): lax.dot_general(rows_part, trail_view, (((1,), (1,)), ((), ())), precisio...]
    unnamed x104 -> x4, local copies, waits for them, and re-layouts: 83.6 us -> 3.51 us
    reshape x24 -> x0, local copies, waits for them, and re-layouts: 72.3 us -> none  [local_part(): gathered.reshape(row_procs, row_blocks, blk_size, blk_size)]
  transfers between devices with their start and end apart: 72 -> 0, of which waited for: 71 -> 0; matrix products, arithmetic and copies ran while one was open for 2% -> 0% of each run, Pallas kernels for 0% -> 0%
where the time goes in v1:
time: 398 us; the launch traced here: 392 us
  Pallas kernels  388 us (97%)
    pallas_call x1, Pallas kernels, local_part(): pl.pallas_call(make_kernel(row_procs, col_procs, local_rows, panel_dev),...  388 us

profile of v1, /device:TPU:7, one launch (start us, length us, event | category | flops | bytes accessed | tf_op | source)
XLA Modules:
  0.0 392.0 jit_solution(3752471074320157155)
XLA Ops:
  0.6 387.8 %shard_map.41 = (f32[3,1024,128]{2,1,0:T(8,128)}, f32[1024,128]{1,0:T(8,128)}) custom-call(f32[3,1024,128]{2,1,0:T(8,128)} %bitcast.3, f32[1024,128]{1,0:T(8,128)} %trl_in.1), custom_call_target="tpu_custom_call" | custom-call | tf_op jit(solution)/shard_map/pallas_call | solution.py:495
  388.5 0.0 copy-start
  388.5 2.7 copy.6
  391.2 0.0 copy-done
  391.2 0.8 copy.7
Async XLA Ops:
  388.5 2.7 copy-start

commit v2 on v1

--- a/solution.py
+++ b/solution.py
@@ -95,9 +95,9 @@
     half = row_blocks // 2
     sib_row = CHAIN_ROW ^ 1
 
-    def kernel(pan_in, trl_in, pan_out, trl_out, tile, rowp, colp, linv_in, ldiag_in, stage, win, lwin, linv_c, lt_c, diag,
-               in_sem, row_sem, col_sem, linv_sem, ldiag_sem, win_sem, outc_sem, out_sem,
-               row_snd, col_snd, stage_snd, init_snd, linv_snd, ldiag_snd, give_snd, give_sem):
+    def kernel(pan_in, trl_in, pan_out, trl_out, tile, rowp, colp, linv_in, lnext_in, ldiag_in, stage, win, lwin, linv_c, lt_c, diag,
+               in_sem, row_sem, col_sem, linv_sem, lnext_sem, ldiag_sem, win_sem, outc_sem, out_sem,
+               row_snd, col_snd, stage_snd, init_snd, linv_snd, lnext_snd, ldiag_snd, give_snd, give_sem):
         pc = lax.axis_index("pc")
         pr = lax.axis_index("pr")
         at_chain_col = pc == CHAIN_COL
@@ -148,6 +148,10 @@
         def linv_goes(i, r):
             return jnp.logical_or(lax.rem(i, col_procs) != CHAIN_COL, r != CHAIN_ROW)
 
+        def lnext_copy(i, r):
+            return remote(lwin.at[lax.rem(i, RING), LAG - 1], lnext_in.at[i // col_procs], lnext_snd.at[lax.rem(i, 2), r],
+                          lnext_sem.at[i // col_procs], (lax.rem(i, col_procs), r))
+
         def ldiag_copy(i):
             return remote(lt_c.at[i], ldiag_in.at[i // col_procs], ldiag_snd.at[lax.rem(i, 2)], ldiag_sem.at[i // col_procs],
                           (lax.rem(i, col_procs), lax.rem(i, row_procs)))
@@ -157,6 +161,10 @@
                 @pl.when(linv_goes(i, r))
                 def _():
                     linv_copy(i, r).wait_send()
+
+                    @pl.when(i >= 1)
+                    def _():
+                        lnext_copy(i, r).wait_send()
             ldiag_copy(i).wait_send()
 
         def chain_step(i, _):
@@ -192,6 +200,10 @@
                 @pl.when(linv_goes(i, r))
                 def _():
                     linv_copy(i, r).start()
+
+                    @pl.when(i >= 1)
+                    def _():
+                        lnext_copy(i, r).start()
             ldiag_copy(i).start()
             return 0
 
@@ -239,18 +251,22 @@
             moved = jnp.logical_and(peer == CHAIN_COL, r == CHAIN_ROW)
             v_dst = jnp.where(moved, 1, 0)
             r_dst = jnp.where(moved, sib_row, r)
-            return remote(rowp.at[v, k, rows(l)], rowp.at[v_dst, k, rows(l)], row_snd.at[lax.rem(k, 2), v, l, c],
+            return remote(rowp.at[v, k, rows(l)], rowp.at[v_dst, k, rows(l)], row_snd.at[lax.rem(k, 3), v, l, c],
                           row_sem.at[v_dst, k, l], (peer, r_dst))
 
         def col_copy(k, v, l, m, d):
-            return remote(rowp.at[v, k, rows(l)], colp.at[k, rows(m)], col_snd.at[lax.rem(k, 2), m, d - 1],
+            return remote(rowp.at[v, k, rows(l)], colp.at[k, rows(m)], col_snd.at[lax.rem(k, 3), m, d - 1],
                           col_sem.at[k, m], (pc, lax.rem(pr + d, row_procs)))
 
         def col_goes(d):
             return jnp.logical_not(jnp.logical_and(at_chain_col, lax.rem(pr + d, row_procs) == CHAIN_ROW))
 
-        def is_col_block(v, l):
-            return jnp.logical_and(row_of(v) == lax.rem(pc, row_procs), lax.rem(l, 2) == col_half)
+        def needs_col(k, col_block):
+            return jnp.logical_and(col_block > k, jnp.logical_or(col_block != k + 1, col_block >= steps))
+
+        def is_col_block(k, v, l):
+            here = jnp.logical_and(row_of(v) == lax.rem(pc, row_procs), lax.rem(l, 2) == col_half)
+            return jnp.logical_and(here, needs_col(k, pc + (l // 2) * col_procs))
 
         def each_block(k, act):
             def virtual(v, _):
@@ -266,7 +282,7 @@
                 def _():
                     act(row_copy(k, v, l, c, peer))
 
-            @pl.when(is_col_block(v, l))
+            @pl.when(is_col_block(k, v, l))
             def _():
                 for d in range(1, row_procs):
                     @pl.when(col_goes(d))
@@ -307,80 +323,142 @@
             def _():
                 out_remote(m).start()
 
+        has_src = jnp.logical_or(is_col_src, jnp.logical_and(is_sib, CHAIN_ROW == lax.rem(pc, row_procs)))
+
+        def wait_col(k, m):
+            wait_recv(colp.at[k, rows(m)], col_sem.at[k, m])
+
+        def entered_slot(k):
+            slot = jnp.int32(-1)
+            for v in range(2):
+                here, i, s, m = entering(k, v)
+                here = jnp.logical_and(jnp.logical_and(here, s > 0), jnp.logical_and(v < num_virtual, k >= 0))
+                slot = jnp.where(here, m, slot)
+            return slot
+
+        def send_block(k, v, l):
+            each_send(k, v, l, lambda c: c.start())
+
+            @pl.when(is_col_block(k, v, l))
+            def _():
+                colp[k, rows(l // 2), :] = rowp[v, k, rows(l), :]
+
+        def enter(k, v):
+            here, i, s, m = entering(k, v)
+
+            @pl.when(jnp.logical_and(here, s > 0))
+            def _():
+                @pl.when(jnp.logical_not(has_src))
+                def _():
+                    wait_col(k, m)
+
+                l = i // row_procs
+                new = tile[v, m, rows(l), :] - dot_nt(rowp[v, k, rows(l), :], colp[k, rows(m), :])
+                tile[v, m, rows(l), :] = new
+                stage[v, l] = new
+                stage_copy(v, i, s).start()
+
+        def solve_next(k, v, l, first):
+            m = (k + 1) // col_procs
+            i = row_procs * l + row_of(v)
+            new = tile[v, m, rows(l), :]
+            if not first:
+                prev = jnp.maximum(k - 1, 0)
+                old = dot_nt(rowp[v, prev, rows(l), :], colp[prev, rows(m), :])
+                skip = jnp.logical_or(k == 0, jnp.logical_and(i == k + LAG, i < steps))
+                new = new - jnp.where(skip, 0.0, old)
+                new = new - dot_nt(rowp[v, k, rows(l), :], lnext_in[m])
+
+                @pl.when(jnp.logical_and(i == k + LAG + 1, i < steps))
+                def _():
+                    stage[v, l] = new
+                    stage_copy(v, i, 0).start()
+            x = dot_nt(new, linv_in[m])
+            rowp[v, k + 1, rows(l), :] = x
+            tile[v, m, rows(l), :] = x
+            send_block(k + 1, v, l)
+
+        def update_row(q, v, l):
+            r = row_of(v)
+            i_row = row_procs * l + r
+            upd = dot_nt(rowp[v, q, rows(l), :], colp[q])
+            entered = jnp.logical_and(i_row == q + LAG + 1, i_row < steps)
+            for m in range(slots):
+                col_block = pc + m * col_procs
+                take = jnp.logical_and(col_block > q, jnp.logical_or(col_block > q + 2, col_block >= steps))
+                take = jnp.logical_and(take, jnp.logical_not(jnp.logical_and(entered, col_block <= i_row)))
+                if m < panel_dev:
+                    take = jnp.logical_and(take, i_row >= col_block)
+
+                @pl.when(take)
+                def _():
+                    tile[v, m, rows(l), :] = tile[v, m, rows(l), :] - upd[:, m * NB:(m + 1) * NB]
+
         def owner_step(k, _):
-            own = pc == lax.rem(k, col_procs)
+            own = jnp.logical_and(pc == lax.rem(k, col_procs), k < steps)
+            own_next = jnp.logical_and(pc == lax.rem(k + 1, col_procs), k + 1 < steps)
             m_own = k // col_procs
+            m_next = (k + 1) // col_procs
+            entered_before = entered_slot(k - 1)
 
             @pl.when(k >= 2)
             def _():
                 drain_sends(k - 2)
 
-            @pl.when(own)
-            def _():
-                wait_recv(linv_in.at[m_own], linv_sem.at[m_own])
-
-            def panel(v, l):
-                @pl.when(own)
-                def _():
-                    x = dot_nt(tile[v, m_own, rows(l), :], linv_in[m_own])
-                    rowp[v, k, rows(l), :] = x
-                    tile[v, m_own, rows(l), :] = x
-
-                @pl.when(jnp.logical_not(own))
-                def _():
-                    wait_recv(rowp.at[v, k, rows(l)], row_sem.at[v, k, l])
-
-                each_send(k, v, l, lambda c: c.start())
-
-                @pl.when(is_col_block(v, l))
-                def _():
-                    colp[k, rows(l // 2), :] = rowp[v, k, rows(l), :]
-
-            each_block(k, panel)
-
-            has_src = jnp.logical_or(is_col_src, jnp.logical_and(is_sib, CHAIN_ROW == lax.rem(pc, row_procs)))
-            for m in range(slots):
-                @pl.when(jnp.logical_and(jnp.logical_not(has_src), pc + m * col_procs > k))
-                def _():
-                    wait_recv(colp.at[k, m * NB:(m + 1) * NB], col_sem.at[k, m])
-
-            def enter(v, _):
-                here, i, s, m = entering(k, v)
-
-                @pl.when(here)
-                def _():
-                    l = i // row_procs
-                    new = tile[v, m, rows(l), :] - dot_nt(rowp[v, k, rows(l), :], colp[k, rows(m), :])
-                    tile[v, m, rows(l), :] = new
-                    stage[v, l] = new
-                    stage_copy(v, i, s).start()
+            @pl.when(own_next)
+            def _():
+                wait_recv(linv_in.at[m_next], linv_sem.at[m_next])
+                wait_recv(lnext_in.at[m_next], lnext_sem.at[m_next])
+
+                @pl.when(jnp.logical_and(jnp.logical_not(has_src), jnp.logical_and(k >= 1, entered_before != m_next)))
+                def _():
+                    wait_col(k - 1, m_next)
+
+            def row(t, _):
+                @pl.when(jnp.logical_and(t == 2, k >= 1))
+                def _():
+                    for m in range(slots):
+                        col_block = pc + m * col_procs
+                        due = jnp.logical_and(needs_col(k - 1, col_block), entered_before != m)
+                        due = jnp.logical_and(due, jnp.logical_not(jnp.logical_and(own_next, m == m_next)))
+
+                        @pl.when(jnp.logical_and(due, jnp.logical_not(has_src)))
+                        def _():
+                            wait_col(k - 1, m)
+
+                def virtual(v, _):
+                    r = row_of(v)
+                    l = k // row_procs + t
+
+                    @pl.when(jnp.logical_and(jnp.logical_and(l < row_blocks, l >= first_block(k, r)), k < steps))
+                    def _():
+                        @pl.when(jnp.logical_not(own))
+                        def _():
+                            wait_recv(rowp.at[v, k, rows(l)], row_sem.at[v, k, l])
+                            send_block(k, v, l)
+
+                        @pl.when(jnp.logical_and(own_next, row_procs * l + r > k + 1))
+                        def _():
+                            solve_next(k, v, l, False)
+
+                    l_upd = l - 2
+
+                    @pl.when(jnp.logical_and(jnp.logical_and(t >= 2, k >= 1), l_upd >= first_block(k - 1, r)))
+                    def _():
+                        update_row(k - 1, v, l_upd)
+                    return 0
+
+                return lax.fori_loop(0, num_virtual, virtual, 0)
+
+            lax.fori_loop(0, row_blocks + 2 - k // row_procs, row, 0)
+
+            def end_of_row(v, _):
+                @pl.when(k < steps)
+                def _():
+                    enter(k, v)
                 return 0
 
-            lax.fori_loop(0, num_virtual, enter, 0)
-
-            def update(v, _):
-                r = row_of(v)
-                here, i, s, m_in = entering(k, v)
-                l_in = jnp.where(here, i // row_procs, -1)
-                first = first_block(k, r)
-                for m in range(slots):
-                    col_block = pc + m * col_procs
-                    low = first
-                    if m < panel_dev:
-                        low = jnp.maximum(first, (col_block - r + row_procs - 1) // row_procs)
-                    for h in range(2):
-                        @pl.when(jnp.logical_and(col_block > k, low < (h + 1) * half))
-                        def _():
-                            part = pl.ds(h * half * NB, half * NB)
-                            upd = dot_nt(rowp[v, k, part, :], colp[k, m * NB:(m + 1) * NB, :])
-                            for b in range(half):
-                                l = h * half + b
-                                take = jnp.logical_and(l >= low, jnp.logical_or(m_in != m, l_in != l))
-                                blk = slice(l * NB, (l + 1) * NB)
-                                tile[v, m, blk, :] = tile[v, m, blk, :] - jnp.where(take, upd[b * NB:(b + 1) * NB], 0.0)
-                return 0
-
-            lax.fori_loop(0, num_virtual, update, 0)
+            lax.fori_loop(0, num_virtual, end_of_row, 0)
 
             @pl.when(own)
             def _():
@@ -405,6 +483,16 @@
                     def _():
                         start_out(m)
             return 0
+
+        def first_column():
+            wait_recv(linv_in.at[0], linv_sem.at[0])
+
+            def virtual(v, _):
+                def block(l, _):
+                    solve_next(-1, v, l, True)
+                    return 0
+                return lax.fori_loop(first_block(0, row_of(v)), row_blocks, block, 0)
+            lax.fori_loop(0, num_virtual, virtual, 0)
 
         @pl.when(jnp.logical_not(is_chain))
         def _():
@@ -420,9 +508,12 @@
                 for m in range(slots):
                     wait_recv(tile.at[1, m], give_sem.at[m])
 
-            lax.fori_loop(0, steps, owner_step, 0)
+            @pl.when(pc == 0)
+            def _():
+                first_column()
+
+            lax.fori_loop(0, steps + 1, owner_step, 0)
             start_out(panel_dev)
-            drain_sends(steps - 2)
             drain_sends(steps - 1)
             for i in range(LAG + 1):
                 @pl.when(init_goes(i))
@@ -467,6 +558,7 @@
             pltpu.VMEM((steps, slots * NB, NB), f32),
             pltpu.VMEM((panel_dev, NB, NB), f32),
             pltpu.VMEM((panel_dev, NB, NB), f32),
+            pltpu.VMEM((panel_dev, NB, NB), f32),
             pltpu.VMEM((2, steps // row_procs, NB, NB), f32),
             pltpu.VMEM((steps, LAG + 1, NB, NB), f32),
             pltpu.VMEM((RING, LAG, NB, NB), f32),
@@ -478,13 +570,15 @@
             dma((steps, slots)),
             dma((panel_dev,)),
             dma((panel_dev,)),
+            dma((panel_dev,)),
             dma((steps, LAG + 1)),
             dma((slots,)),
             dma((2 * slots,)),
-            dma((2, 2, row_blocks, 3)),
-            dma((2, slots, row_procs - 1)),
+            dma((3, 2, row_blocks, 3)),
+            dma((3, slots, row_procs - 1)),
             dma((2, steps // row_procs)),
             dma((LAG + 1,)),
+            dma((2, row_procs)),
             dma((2, row_procs)),
             dma((2,)),
             dma((slots,)),

time: 398 us -> 347 us (0.87); the launches traced: 392 us -> 347 us
  Pallas kernels: 388 us -> 342 us
    pallas_call x1, Pallas kernels: 388 us -> 342 us  [local_part(): pl.pallas_call(make_kernel(row_procs, col_procs, local_rows, panel_dev),...]
where the time goes in v2:
time: 347 us
  Pallas kernels  342 us (99%)
  local copies, waits for them, and re-layouts  3.51 us (1%)
    pallas_call x1, Pallas kernels, local_part(): pl.pallas_call(make_kernel(row_procs, col_procs, local_rows, panel_dev),...  342 us

profile of v2, /device:TPU:7, one launch (start us, length us, event | category | flops | bytes accessed | tf_op | source)
XLA Modules:
  0.0 346.6 jit_solution(7769611659519935618)
XLA Ops:
  0.6 342.4 %shard_map.41 = (f32[3,1024,128]{2,1,0:T(8,128)}, f32[1024,128]{1,0:T(8,128)}) custom-call(f32[3,1024,128]{2,1,0:T(8,128)} %bitcast.3, f32[1024,128]{1,0:T(8,128)} %trl_in.1), custom_call_target="tpu_custom_call" | custom-call | tf_op jit(solution)/shard_map/pallas_call | solution.py:589
  343.1 0.0 copy-start
  343.1 2.7 copy.6
  345.8 0.0 copy-done
  345.8 0.8 copy.7
Async XLA Ops:
  343.1 2.7 copy-start

commit v3 on v2

--- a/solution.py
+++ b/solution.py
@@ -240,11 +240,28 @@
 
         def row_children(k):
             owner = lax.rem(k, col_procs)
+            follows = jnp.where(k + 1 < steps, lax.rem(k + 1, col_procs), -1)
             z_own, y_own = owner // 2, lax.rem(owner, 2)
-            to_y = pc == owner
-            to_up = jnp.logical_and(z_me >= z_own, z_me < col_procs // 2 - 1)
-            to_down = jnp.logical_and(z_me <= z_own, z_me > 0)
-            return ((to_y, z_me * 2 + 1 - y_me), (to_up, pc + 2), (to_down, pc - 2))
+            y_far = 1 - y_own
+            z_by = jnp.where(z_own < col_procs // 2 - 1, z_own + 1, z_own - 1)
+
+            def parents(peer):
+                z, y = peer // 2, lax.rem(peer, 2)
+                inward = jnp.where(z < z_own, z + 1, z - 1)
+                in_line = y == y_own
+                even = jnp.where(in_line, inward * 2 + y, jnp.where(z == z_own, z_by * 2 + y, z * 2 + y_own))
+                odd = jnp.where(in_line, z * 2 + y_far, jnp.where(z == z_own, owner, inward * 2 + y))
+                first = peer == follows
+                return jnp.where(first, owner, even), jnp.where(first, owner, odd)
+
+            found = []
+            for peer, valid in ((z_me * 2 + 1 - y_me, True), (pc + 2, z_me < col_procs // 2 - 1), (pc - 2, z_me > 0)):
+                ok = jnp.logical_and(valid, peer != owner)
+                even, odd = parents(jnp.maximum(peer, 0))
+                found.append((jnp.logical_and(ok, even == pc), jnp.logical_and(ok, odd == pc), peer))
+            jump = jnp.logical_and(jnp.logical_and(pc == owner, y_own == 1), follows >= 0)
+            found.append((jump, jump, jnp.maximum(follows, 0)))
+            return found
 
         def row_copy(k, v, l, c, peer):
             r = row_of(v)
@@ -276,9 +293,10 @@
                 return lax.fori_loop(first_block(k, row_of(v)), row_blocks, block, 0)
             lax.fori_loop(0, num_virtual, virtual, 0)
 
-        def each_send(k, v, l, act):
-            for c, (goes, peer) in enumerate(row_children(k)):
-                @pl.when(goes)
+        def each_send(k, v, l, act, children):
+            odd_row = lax.rem(l, 2) == 1
+            for c, (even, odd, peer) in enumerate(children):
+                @pl.when(jnp.where(odd_row, odd, even))
                 def _():
                     act(row_copy(k, v, l, c, peer))
 
@@ -290,7 +308,8 @@
                         act(col_copy(k, v, l, l // 2, d))
 
         def drain_sends(k):
-            each_block(k, lambda v, l: each_send(k, v, l, lambda c: c.wait_send()))
+            children = row_children(k)
+            each_block(k, lambda v, l: each_send(k, v, l, lambda c: c.wait_send(), children))
 
         def stage_copy(v, i, s):
             return remote(stage.at[v, i // row_procs], win.at[i, s], stage_snd.at[v, i // row_procs], win_sem.at[i, s], chain_id)
@@ -336,8 +355,8 @@
                 slot = jnp.where(here, m, slot)
             return slot
 
-        def send_block(k, v, l):
-            each_send(k, v, l, lambda c: c.start())
+        def send_block(k, v, l, children):
+            each_send(k, v, l, lambda c: c.start(), children)
 
             @pl.when(is_col_block(k, v, l))
             def _():
@@ -358,16 +377,16 @@
                 stage[v, l] = new
                 stage_copy(v, i, s).start()
 
-        def solve_next(k, v, l, first):
+        def solve_next(k, v, l, first, children):
             m = (k + 1) // col_procs
             i = row_procs * l + row_of(v)
             new = tile[v, m, rows(l), :]
             if not first:
                 prev = jnp.maximum(k - 1, 0)
-                old = dot_nt(rowp[v, prev, rows(l), :], colp[prev, rows(m), :])
                 skip = jnp.logical_or(k == 0, jnp.logical_and(i == k + LAG, i < steps))
-                new = new - jnp.where(skip, 0.0, old)
-                new = new - dot_nt(rowp[v, k, rows(l), :], lnext_in[m])
+                left = jnp.concatenate([jnp.where(skip, 0.0, rowp[v, prev, rows(l), :]), rowp[v, k, rows(l), :]], axis=1)
+                right = jnp.concatenate([jnp.where(k == 0, 0.0, colp[prev, rows(m), :]), lnext_in[m]], axis=1)
+                new = new - dot_nt(left, right)
 
                 @pl.when(jnp.logical_and(i == k + LAG + 1, i < steps))
                 def _():
@@ -376,7 +395,7 @@
             x = dot_nt(new, linv_in[m])
             rowp[v, k + 1, rows(l), :] = x
             tile[v, m, rows(l), :] = x
-            send_block(k + 1, v, l)
+            send_block(k + 1, v, l, children)
 
         def update_row(q, v, l):
             r = row_of(v)
@@ -400,6 +419,8 @@
             m_own = k // col_procs
             m_next = (k + 1) // col_procs
             entered_before = entered_slot(k - 1)
+            children = row_children(k)
+            children_next = row_children(k + 1)
 
             @pl.when(k >= 2)
             def _():
@@ -435,11 +456,11 @@
                         @pl.when(jnp.logical_not(own))
                         def _():
                             wait_recv(rowp.at[v, k, rows(l)], row_sem.at[v, k, l])
-                            send_block(k, v, l)
+                            send_block(k, v, l, children)
 
                         @pl.when(jnp.logical_and(own_next, row_procs * l + r > k + 1))
                         def _():
-                            solve_next(k, v, l, False)
+                            solve_next(k, v, l, False, children_next)
 
                     l_upd = l - 2
 
@@ -486,10 +507,11 @@
 
         def first_column():
             wait_recv(linv_in.at[0], linv_sem.at[0])
+            children = row_children(0)
 
             def virtual(v, _):
                 def block(l, _):
-                    solve_next(-1, v, l, True)
+                    solve_next(-1, v, l, True, children)
                     return 0
                 return lax.fori_loop(first_block(0, row_of(v)), row_blocks, block, 0)
             lax.fori_loop(0, num_virtual, virtual, 0)
@@ -574,7 +596,7 @@
             dma((steps, LAG + 1)),
             dma((slots,)),
             dma((2 * slots,)),
-            dma((3, 2, row_blocks, 3)),
+            dma((3, 2, row_blocks, 4)),
             dma((3, slots, row_procs - 1)),
             dma((2, steps // row_procs)),
             dma((LAG + 1,)),

time: 347 us -> 576 us (1.66)
  Pallas kernels: 342 us -> 568 us
    pallas_call x1, Pallas kernels: 342 us -> 568 us  [local_part(): pl.pallas_call(make_kernel(row_procs, col_procs, local_rows, panel_dev),...]
where the time goes in v3:
time: 576 us; the launch traced here: 572 us
  Pallas kernels  568 us (99%)
    pallas_call x1, Pallas kernels, local_part(): pl.pallas_call(make_kernel(row_procs, col_procs, local_rows, panel_dev),...  568 us

profile of v3, /device:TPU:7, one launch (start us, length us, event | category | flops | bytes accessed | tf_op | source)
XLA Modules:
  0.0 572.4 jit_solution(11596538939533039004)
XLA Ops:
  0.6 568.2 %shard_map.41 = (f32[3,1024,128]{2,1,0:T(8,128)}, f32[1024,128]{1,0:T(8,128)}) custom-call(f32[3,1024,128]{2,1,0:T(8,128)} %bitcast.3, f32[1024,128]{1,0:T(8,128)} %trl_in.1), custom_call_target="tpu_custom_call" | custom-call | tf_op jit(solution)/shard_map/pallas_call | solution.py:611
  568.9 0.0 copy-start
  568.9 2.7 copy.6
  571.6 0.0 copy-done
  571.6 0.8 copy.7
Async XLA Ops:
  568.9 2.7 copy-start

commit v4 on v3

--- a/solution.py
+++ b/solution.py
@@ -8,10 +8,11 @@
 MESH = pl.DeviceIdType.MESH
 PREC_HIGH = lax.Precision.HIGHEST
 NB = 128
-LAG = 3
+LAG = 4
 CHAIN_COL = 2
 CHAIN_ROW = 1
 RING = 8
+BEHIND = 2
 
 
 def _sub_bcast(v, s):
@@ -240,27 +241,23 @@
 
         def row_children(k):
             owner = lax.rem(k, col_procs)
-            follows = jnp.where(k + 1 < steps, lax.rem(k + 1, col_procs), -1)
             z_own, y_own = owner // 2, lax.rem(owner, 2)
-            y_far = 1 - y_own
-            z_by = jnp.where(z_own < col_procs // 2 - 1, z_own + 1, z_own - 1)
 
             def parents(peer):
                 z, y = peer // 2, lax.rem(peer, 2)
-                inward = jnp.where(z < z_own, z + 1, z - 1)
+                along = jnp.where(z < z_own, z + 1, z - 1) * 2 + y
+                across = z * 2 + 1 - y
                 in_line = y == y_own
-                even = jnp.where(in_line, inward * 2 + y, jnp.where(z == z_own, z_by * 2 + y, z * 2 + y_own))
-                odd = jnp.where(in_line, z * 2 + y_far, jnp.where(z == z_own, owner, inward * 2 + y))
-                first = peer == follows
-                return jnp.where(first, owner, even), jnp.where(first, owner, odd)
+                at_own = z == z_own
+                even = jnp.where(at_own, owner, jnp.where(in_line, along, across))
+                odd = jnp.where(at_own, owner, jnp.where(in_line, across, along))
+                return even, odd
 
             found = []
             for peer, valid in ((z_me * 2 + 1 - y_me, True), (pc + 2, z_me < col_procs // 2 - 1), (pc - 2, z_me > 0)):
                 ok = jnp.logical_and(valid, peer != owner)
                 even, odd = parents(jnp.maximum(peer, 0))
                 found.append((jnp.logical_and(ok, even == pc), jnp.logical_and(ok, odd == pc), peer))
-            jump = jnp.logical_and(jnp.logical_and(pc == owner, y_own == 1), follows >= 0)
-            found.append((jump, jump, jnp.maximum(follows, 0)))
             return found
 
         def row_copy(k, v, l, c, peer):
@@ -294,7 +291,7 @@
             lax.fori_loop(0, num_virtual, virtual, 0)
 
         def each_send(k, v, l, act, children):
-            odd_row = lax.rem(l, 2) == 1
+            odd_row = lax.rem(row_of(v), 2) == 1
             for c, (even, odd, peer) in enumerate(children):
                 @pl.when(jnp.where(odd_row, odd, even))
                 def _():
@@ -347,14 +344,6 @@
         def wait_col(k, m):
             wait_recv(colp.at[k, rows(m)], col_sem.at[k, m])
 
-        def entered_slot(k):
-            slot = jnp.int32(-1)
-            for v in range(2):
-                here, i, s, m = entering(k, v)
-                here = jnp.logical_and(jnp.logical_and(here, s > 0), jnp.logical_and(v < num_virtual, k >= 0))
-                slot = jnp.where(here, m, slot)
-            return slot
-
         def send_block(k, v, l, children):
             each_send(k, v, l, lambda c: c.start(), children)
 
@@ -365,12 +354,8 @@
         def enter(k, v):
             here, i, s, m = entering(k, v)
 
-            @pl.when(jnp.logical_and(here, s > 0))
-            def _():
-                @pl.when(jnp.logical_not(has_src))
-                def _():
-                    wait_col(k, m)
-
+            @pl.when(jnp.logical_and(here, s > 1))
+            def _():
                 l = i // row_procs
                 new = tile[v, m, rows(l), :] - dot_nt(rowp[v, k, rows(l), :], colp[k, rows(m), :])
                 tile[v, m, rows(l), :] = new
@@ -383,8 +368,12 @@
             new = tile[v, m, rows(l), :]
             if not first:
                 prev = jnp.maximum(k - 1, 0)
-                skip = jnp.logical_or(k == 0, jnp.logical_and(i == k + LAG, i < steps))
-                left = jnp.concatenate([jnp.where(skip, 0.0, rowp[v, prev, rows(l), :]), rowp[v, k, rows(l), :]], axis=1)
+                @pl.when(jnp.logical_and(k >= 1, jnp.logical_and(i == k + LAG, i < steps)))
+                def _():
+                    stage[v, l] = tile[v, m, rows(l), :] - dot_nt(rowp[v, prev, rows(l), :], colp[prev, rows(m), :])
+                    stage_copy(v, i, 1).start()
+
+                left = jnp.concatenate([jnp.where(k == 0, 0.0, rowp[v, prev, rows(l), :]), rowp[v, k, rows(l), :]], axis=1)
                 right = jnp.concatenate([jnp.where(k == 0, 0.0, colp[prev, rows(m), :]), lnext_in[m]], axis=1)
                 new = new - dot_nt(left, right)
 
@@ -418,7 +407,6 @@
             own_next = jnp.logical_and(pc == lax.rem(k + 1, col_procs), k + 1 < steps)
             m_own = k // col_procs
             m_next = (k + 1) // col_procs
-            entered_before = entered_slot(k - 1)
             children = row_children(k)
             children_next = row_children(k + 1)
 
@@ -431,21 +419,26 @@
                 wait_recv(linv_in.at[m_next], linv_sem.at[m_next])
                 wait_recv(lnext_in.at[m_next], lnext_sem.at[m_next])
 
-                @pl.when(jnp.logical_and(jnp.logical_not(has_src), jnp.logical_and(k >= 1, entered_before != m_next)))
+                @pl.when(jnp.logical_and(jnp.logical_not(has_src), k >= 1))
                 def _():
                     wait_col(k - 1, m_next)
 
             def row(t, _):
-                @pl.when(jnp.logical_and(t == 2, k >= 1))
+                @pl.when(jnp.logical_and(t == BEHIND, k >= 1))
                 def _():
                     for m in range(slots):
                         col_block = pc + m * col_procs
-                        due = jnp.logical_and(needs_col(k - 1, col_block), entered_before != m)
-                        due = jnp.logical_and(due, jnp.logical_not(jnp.logical_and(own_next, m == m_next)))
+                        due = jnp.logical_and(needs_col(k - 1, col_block), jnp.logical_not(jnp.logical_and(own_next, m == m_next)))
 
                         @pl.when(jnp.logical_and(due, jnp.logical_not(has_src)))
                         def _():
                             wait_col(k - 1, m)
+
+                    def window(v, _):
+                        enter(k - 1, v)
+                        return 0
+
+                    lax.fori_loop(0, num_virtual, window, 0)
 
                 def virtual(v, _):
                     r = row_of(v)
@@ -462,24 +455,16 @@
                         def _():
                             solve_next(k, v, l, False, children_next)
 
-                    l_upd = l - 2
-
-                    @pl.when(jnp.logical_and(jnp.logical_and(t >= 2, k >= 1), l_upd >= first_block(k - 1, r)))
+                    l_upd = l - BEHIND
+
+                    @pl.when(jnp.logical_and(jnp.logical_and(t >= BEHIND, k >= 1), l_upd >= first_block(k - 1, r)))
                     def _():
                         update_row(k - 1, v, l_upd)
                     return 0
 
                 return lax.fori_loop(0, num_virtual, virtual, 0)
 
-            lax.fori_loop(0, row_blocks + 2 - k // row_procs, row, 0)
-
-            def end_of_row(v, _):
-                @pl.when(k < steps)
-                def _():
-                    enter(k, v)
-                return 0
-
-            lax.fori_loop(0, num_virtual, end_of_row, 0)
+            lax.fori_loop(0, row_blocks + BEHIND - k // row_procs, row, 0)
 
             @pl.when(own)
             def _():
@@ -596,7 +581,7 @@
             dma((steps, LAG + 1)),
             dma((slots,)),
             dma((2 * slots,)),
-            dma((3, 2, row_blocks, 4)),
+            dma((3, 2, row_blocks, 3)),
             dma((3, slots, row_procs - 1)),
             dma((2, steps // row_procs)),
             dma((LAG + 1,)),

time: 576 us -> 405 us (0.70)
  Pallas kernels: 568 us -> 401 us
    pallas_call x1, Pallas kernels: 568 us -> 401 us  [local_part(): pl.pallas_call(make_kernel(row_procs, col_procs, local_rows, panel_dev),...]
where the time goes in v4:
time: 405 us
  Pallas kernels  401 us (99%)
    pallas_call x1, Pallas kernels, local_part(): pl.pallas_call(make_kernel(row_procs, col_procs, local_rows, panel_dev),...  401 us

profile of v4, /device:TPU:7, one launch (start us, length us, event | category | flops | bytes accessed | tf_op | source)
XLA Modules:
  0.0 404.9 jit_solution(4450140036598906055)
XLA Ops:
  0.6 400.8 %shard_map.41 = (f32[3,1024,128]{2,1,0:T(8,128)}, f32[1024,128]{1,0:T(8,128)}) custom-call(f32[3,1024,128]{2,1,0:T(8,128)} %bitcast.3, f32[1024,128]{1,0:T(8,128)} %trl_in.1), custom_call_target="tpu_custom_call" | custom-call | tf_op jit(solution)/shard_map/pallas_call | solution.py:596
  401.4 0.0 copy-start
  401.4 2.7 copy.6
  404.1 0.0 copy-done
  404.1 0.8 copy.7
Async XLA Ops:
  401.4 2.7 copy-start

commit v5 on v4

--- a/solution.py
+++ b/solution.py
@@ -9,10 +9,11 @@
 PREC_HIGH = lax.Precision.HIGHEST
 NB = 128
 LAG = 4
-CHAIN_COL = 2
+CHAIN_COL = 4
 CHAIN_ROW = 1
 RING = 8
 BEHIND = 2
+PIECES = 1
 
 
 def _sub_bcast(v, s):
@@ -111,6 +112,9 @@
         def rows(l):
             return pl.ds(pl.multiple_of(l * NB, NB), NB)
 
+        def piece(l, h):
+            return pl.ds(pl.multiple_of(l * NB + h * (NB // PIECES), NB // PIECES), NB // PIECES)
+
         def remote(src, dst, snd, rcv, dev):
             return pltpu.make_async_remote_copy(src_ref=src, dst_ref=dst, send_sem=snd, recv_sem=rcv, device_id=dev, device_id_type=MESH)
 
@@ -241,32 +245,25 @@
 
         def row_children(k):
             owner = lax.rem(k, col_procs)
-            z_own, y_own = owner // 2, lax.rem(owner, 2)
-
-            def parents(peer):
+            z_own = owner // 2
+
+            def parent(peer):
                 z, y = peer // 2, lax.rem(peer, 2)
-                along = jnp.where(z < z_own, z + 1, z - 1) * 2 + y
-                across = z * 2 + 1 - y
-                in_line = y == y_own
-                at_own = z == z_own
-                even = jnp.where(at_own, owner, jnp.where(in_line, along, across))
-                odd = jnp.where(at_own, owner, jnp.where(in_line, across, along))
-                return even, odd
+                return jnp.where(z == z_own, owner, jnp.where(z < z_own, z + 1, z - 1) * 2 + y)
 
             found = []
             for peer, valid in ((z_me * 2 + 1 - y_me, True), (pc + 2, z_me < col_procs // 2 - 1), (pc - 2, z_me > 0)):
                 ok = jnp.logical_and(valid, peer != owner)
-                even, odd = parents(jnp.maximum(peer, 0))
-                found.append((jnp.logical_and(ok, even == pc), jnp.logical_and(ok, odd == pc), peer))
+                found.append((jnp.logical_and(ok, parent(jnp.maximum(peer, 0)) == pc), peer))
             return found
 
-        def row_copy(k, v, l, c, peer):
+        def row_copy(k, v, l, h, c, peer):
             r = row_of(v)
             moved = jnp.logical_and(peer == CHAIN_COL, r == CHAIN_ROW)
             v_dst = jnp.where(moved, 1, 0)
             r_dst = jnp.where(moved, sib_row, r)
-            return remote(rowp.at[v, k, rows(l)], rowp.at[v_dst, k, rows(l)], row_snd.at[lax.rem(k, 3), v, l, c],
-                          row_sem.at[v_dst, k, l], (peer, r_dst))
+            return remote(rowp.at[v, k, piece(l, h)], rowp.at[v_dst, k, piece(l, h)], row_snd.at[lax.rem(k, 3), v, l * PIECES + h, c],
+                          row_sem.at[v_dst, k, l * PIECES + h], (peer, r_dst))
 
         def col_copy(k, v, l, m, d):
             return remote(rowp.at[v, k, rows(l)], colp.at[k, rows(m)], col_snd.at[lax.rem(k, 3), m, d - 1],
@@ -291,12 +288,17 @@
             lax.fori_loop(0, num_virtual, virtual, 0)
 
         def each_send(k, v, l, act, children):
-            odd_row = lax.rem(row_of(v), 2) == 1
-            for c, (even, odd, peer) in enumerate(children):
-                @pl.when(jnp.where(odd_row, odd, even))
-                def _():
-                    act(row_copy(k, v, l, c, peer))
-
+            for h in range(PIECES):
+                send_piece(k, v, l, h, act, children)
+            send_col(k, v, l, act)
+
+        def send_piece(k, v, l, h, act, children):
+            for c, (goes, peer) in enumerate(children):
+                @pl.when(goes)
+                def _():
+                    act(row_copy(k, v, l, h, c, peer))
+
+        def send_col(k, v, l, act):
             @pl.when(is_col_block(k, v, l))
             def _():
                 for d in range(1, row_procs):
@@ -344,8 +346,8 @@
         def wait_col(k, m):
             wait_recv(colp.at[k, rows(m)], col_sem.at[k, m])
 
-        def send_block(k, v, l, children):
-            each_send(k, v, l, lambda c: c.start(), children)
+        def share_col(k, v, l):
+            send_col(k, v, l, lambda c: c.start())
 
             @pl.when(is_col_block(k, v, l))
             def _():
@@ -384,7 +386,9 @@
             x = dot_nt(new, linv_in[m])
             rowp[v, k + 1, rows(l), :] = x
             tile[v, m, rows(l), :] = x
-            send_block(k + 1, v, l, children)
+            for h in range(PIECES):
+                send_piece(k + 1, v, l, h, lambda c: c.start(), children)
+            share_col(k + 1, v, l)
 
         def update_row(q, v, l):
             r = row_of(v)
@@ -448,8 +452,10 @@
                     def _():
                         @pl.when(jnp.logical_not(own))
                         def _():
-                            wait_recv(rowp.at[v, k, rows(l)], row_sem.at[v, k, l])
-                            send_block(k, v, l, children)
+                            for h in range(PIECES):
+                                wait_recv(rowp.at[v, k, piece(l, h)], row_sem.at[v, k, l * PIECES + h])
+                                send_piece(k, v, l, h, lambda c: c.start(), children)
+                            share_col(k, v, l)
 
                         @pl.when(jnp.logical_and(own_next, row_procs * l + r > k + 1))
                         def _():
@@ -573,7 +579,7 @@
             pltpu.VMEM((steps, NB, NB), f32),
             pltpu.VMEM((NB, NB), f32),
             dma((slots,)),
-            dma((2, steps, row_blocks)),
+            dma((2, steps, row_blocks * PIECES)),
             dma((steps, slots)),
             dma((panel_dev,)),
             dma((panel_dev,)),
@@ -581,7 +587,7 @@
             dma((steps, LAG + 1)),
             dma((slots,)),
             dma((2 * slots,)),
-            dma((3, 2, row_blocks, 3)),
+            dma((3, 2, row_blocks * PIECES, 3)),
             dma((3, slots, row_procs - 1)),
             dma((2, steps // row_procs)),
             dma((LAG + 1,)),

time: 405 us -> 343 us (0.85)
  Pallas kernels: 401 us -> 339 us
    pallas_call x1, Pallas kernels: 401 us -> 339 us  [local_part(): pl.pallas_call(make_kernel(row_procs, col_procs, local_rows, panel_dev),...]
where the time goes in v5:
time: 343 us
  Pallas kernels  339 us (99%)
  local copies, waits for them, and re-layouts  3.51 us (1%)
    pallas_call x1, Pallas kernels, local_part(): pl.pallas_call(make_kernel(row_procs, col_procs, local_rows, panel_dev),...  339 us

profile of v5, /device:TPU:7, one launch (start us, length us, event | category | flops | bytes accessed | tf_op | source)
XLA Modules:
  0.0 343.0 jit_solution(13229694388795059608)
XLA Ops:
  0.6 338.9 %shard_map.41 = (f32[3,1024,128]{2,1,0:T(8,128)}, f32[1024,128]{1,0:T(8,128)}) custom-call(f32[3,1024,128]{2,1,0:T(8,128)} %bitcast.3, f32[1024,128]{1,0:T(8,128)} %trl_in.1), custom_call_target="tpu_custom_call" | custom-call | tf_op jit(solution)/shard_map/pallas_call | solution.py:602
  339.5 0.0 copy-start
  339.5 2.7 copy.6
  342.2 0.0 copy-done
  342.2 0.8 copy.7
Async XLA Ops:
  339.5 2.7 copy-start
